TPU v7x, 32 devices: a whole 2x2x4 slice. The times are simulated.
32 devices in a mesh: seq: 4 (over z), blk: 4 (over y, core), uly: 2 (over x).
Axes of the slice: x: 2, y: 2, z: 4, core: 2. Of those that a mesh axis runs over, the one named last changes fastest.
Arguments:
- queries: bfloat16 [8192, 5120], P(('seq', 'blk', 'uly')), parts along dimension 0, may hold values from -60 to 60, as said below
- keys: bfloat16 [8192, 1024], P(('seq', 'blk', 'uly')), parts along dimension 0, may hold values from -60 to 60, as said below
- values: bfloat16 [8192, 1024], P(('seq', 'blk', 'uly')), parts along dimension 0, may hold values from -6 to 6
- positions: int32 [3, 8192], P(None, ('seq', 'blk', 'uly')), parts along dimension 1, may hold values from 0 to 526
- doc_lengths: int32 [32], P('seq'), parts along dimension 0, may hold values from 1 to 1024, 2048 in all
Outputs:
- attended: bfloat16 [8192, 5120], P(('seq', 'blk', 'uly')), parts along dimension 0
There are 4 independent parts, one for each index of `seq`. A program takes and returns all parts, laid end to end along the dimension named above; each array names one. Nothing has to cross between parts.
Inputs may be any that keep to these rules, and one draw needn't show every extreme that they name: queries; the query rows hold values of order one, a few rows may be much larger. keys; the key rows hold values of order one, a few rows may be much larger.
All inputs are finite; a program needn't handle non-finite values.
Results may differ from a plain program's by a relative error of at most 0.0055.
Values may be sent and summed in bfloat16 or wider, within the bound.
A program may use at most 384 MiB of HBM per device.

v0:
```python
import math

import jax
import jax.numpy as jnp
from jax import lax
from jax.sharding import PartitionSpec as P

HEAD_SIZE = 128
QUERY_PER_KEY = 5


def apply_rotary(x, pos, heads):
    rows = x.shape[0]
    half = HEAD_SIZE // 2
    pair = jnp.arange(half, dtype=jnp.int32)
    freq = jnp.power(jnp.float32(1000000.0), -2.0 * pair.astype(jnp.float32) / HEAD_SIZE)
    place = pos.astype(jnp.float32)
    first = HEAD_SIZE // 8
    second = first + 3 * HEAD_SIZE // 16
    chosen = jnp.where(
        pair[None, :] < first,
        place[0][:, None],
        jnp.where(pair[None, :] < second, place[1][:, None], place[2][:, None]),
    )
    angle = chosen * freq[None, :]
    cosine = jnp.cos(angle)[:, None, :]
    sine = jnp.sin(angle)[:, None, :]
    parts = x.reshape(rows, heads, HEAD_SIZE).astype(jnp.float32)
    lower = parts[..., :half]
    upper = parts[..., half:]
    turned = jnp.concatenate(
        [lower * cosine - upper * sine, upper * cosine + lower * sine], axis=-1
    )
    return turned.reshape(rows, heads * HEAD_SIZE).astype(jnp.bfloat16)


def doc_starts(index, doc_lengths):
    ends = jnp.cumsum(doc_lengths)
    return jnp.sum(jnp.where(ends[None, :] <= index[:, None], doc_lengths[None, :], 0), axis=1)


def attend(rotated, query_index, query_start, kheads, folder):
    rows = rotated.shape[0]
    scale = 1.0 / math.sqrt(HEAD_SIZE)
    grouped_query = rotated.reshape(rows, kheads, QUERY_PER_KEY, HEAD_SIZE)
    last_query = query_index[rows - 1]
    first_start = jnp.min(query_start)

    def update(carry, keys_blk, values_blk, begin):
        best, total, summed = carry
        width = keys_blk.shape[0]
        key_index = begin + jnp.arange(width, dtype=jnp.int32)
        allowed = (key_index[None, :] <= query_index[:, None]) & (
            key_index[None, :] >= query_start[:, None]
        )
        scores = (
            jnp.einsum(
                "rhgd,bhd->hgrb", grouped_query, keys_blk, preferred_element_type=jnp.float32
            )
            * scale
        )
        scores = jnp.where(allowed, scores, -1e30)
        newbest = jnp.maximum(best, jnp.max(scores, axis=-1))
        weights = jnp.where(allowed, jnp.exp(scores - newbest[..., None]), 0.0)
        factor = jnp.exp(best - newbest)
        total = total * factor + jnp.sum(weights, axis=-1)
        summed = summed * factor[..., None] + jnp.einsum(
            "hgrb,bhd->hgrd",
            weights.astype(jnp.bfloat16),
            values_blk,
            preferred_element_type=jnp.float32,
        )
        return (newbest, total, summed)

    def fold_piece(carry, piece, start):
        count = piece.shape[0]
        block = math.gcd(count, 512)

        def step(turn, inner):
            offset = turn * block
            slab = lax.dynamic_slice_in_dim(piece, offset, block, 0)
            keys_blk = slab[:, : kheads * HEAD_SIZE].reshape(block, kheads, HEAD_SIZE)
            values_blk = slab[:, kheads * HEAD_SIZE :].reshape(block, kheads, HEAD_SIZE)
            live = (offset <= last_query) & (offset + block - 1 >= first_start)

            def taken(state):
                return update(state, keys_blk, values_blk, offset)

            def passed(state):
                return state

            return lax.cond(live, taken, passed, inner)

        return lax.fori_loop(0, count // block, step, carry)

    initial = (
        jnp.full((kheads, QUERY_PER_KEY, rows), -1e30, jnp.float32),
        jnp.zeros((kheads, QUERY_PER_KEY, rows), jnp.float32),
        jnp.zeros((kheads, QUERY_PER_KEY, rows, HEAD_SIZE), jnp.float32),
    )
    best, total, summed = folder(fold_piece, initial)
    result = summed / total[..., None]
    return (
        jnp.transpose(result, (2, 0, 1, 3))
        .reshape(rows, kheads * QUERY_PER_KEY * HEAD_SIZE)
        .astype(jnp.bfloat16)
    )


def local(queries, keys, values, positions, doc_lengths):
    rows = queries.shape[0]
    kheads = keys.shape[1] // HEAD_SIZE
    query_rotated = apply_rotary(queries, positions, queries.shape[1] // HEAD_SIZE)
    key_rotated = apply_rotary(keys, positions, kheads)
    index = lax.axis_index(("blk", "uly")) * rows + jnp.arange(rows, dtype=jnp.int32)
    starts = doc_starts(index, doc_lengths)
    paired = jnp.concatenate([key_rotated, values], axis=1)

    def fold_all(fn, init):
        return fn(init, lax.all_gather(paired, ("blk", "uly"), axis=0, tiled=True), jnp.int32(0))

    return attend(query_rotated, index, starts, kheads, fold_all)


def solution(mesh):
    in_specs = (
        P(("seq", "blk", "uly"), None),
        P(("seq", "blk", "uly"), None),
        P(("seq", "blk", "uly"), None),
        P(None, ("seq", "blk", "uly")),
        P("seq"),
    )
    out_specs = P(("seq", "blk", "uly"), None)
    return jax.shard_map(local, mesh=mesh, in_specs=in_specs, out_specs=out_specs, check_vma=False)
```

profile of v0, /device:TPU:13, one launch (start us, length us, event | category | flops | bytes accessed | tf_op | source)
XLA Modules:
  0.0 182.3 jit_solution(12114173742876673106)
XLA Ops:
  6.5 0.0 all-gather.2.cloned.1.call-start
  6.6 0.7 convert_element_type.62
  7.3 0.6 fusion.14
  7.9 0.1 copy.26
  8.0 0.1 copy.28
  8.0 1.2 copy.29
  9.3 1.2 copy.41
  10.5 0.1 subtract_convert_fusion.1
  10.7 0.0 copy-start.2
  10.7 1.1 pad_maximum_fusion.1
  11.8 0.0 all-gather.2.cloned.1.call-update
  11.9 0.7 slice.49
  12.5 0.3 copy-done.2
  12.8 0.6 convert_bitcast_fusion
  13.4 0.0 copy-start.3
  13.4 3.2 %copy.44 = f32[32,8,40,128]{3,2,1,0:T(8,128)} copy(f32[32,8,40,128]{3,1,2,0:T(8,128)S(1)} %convert_bitcast_fusion) | data formatting | bytes 10485760
  16.7 0.0 copy-done.3
  16.7 0.2 reduce-window.8
  16.8 0.1 select_reduce_fusion
  16.9 0.6 reduce_min.9
  17.5 6.3 %fusion.16 = (f32[256,40,64]{2,1,0:T(8,128)S(1)}, f32[256,40,64]{2,1,0:T(8,128)S(1)}) fusion(f32[256,40,128]{2,1,0:T(8,128)} %bitcast.43), kind=kLoop, calls=%fused_computation.36 | loop fusion | bytes 10485760 | tf_op jit(solution)/shard_map/slice | solution.py:29
  23.8 2.1 %subtract_convert_fusion = (bf16[256,40,64]{2,0,1:T(8,128)(2,1)S(1)}, bf16[256,40,64]{2,0,1:T(8,128)(2,1)S(1)}) fusion(f32[256,40,64]{2,1,0:T(8,128)S(1)} %get-tuple-element.497, f32[256,40,64]{2,1,0:T(8,128)S(1)} %get-tuple-element.496, f32[256,64]{1,0:T(8,128)S(1)} %get-tuple-element.501, f32[256,64]{1,0:T(8,128)S(1)} %get-tuple-element.500), kind=kLoop, calls=%fused_computation.21 | loop fusion | flops 5242880 | bytes 7995392 | tf_op jit(solution)/shard_map/convert.2
  25.9 2.9 %pad_maximum_fusion = bf16[256,40,128]{2,0,1:T(8,128)(2,1)} fusion(bf16[256,40,64]{2,0,1:T(8,128)(2,1)S(1)} %get-tuple-element.495, bf16[256,40,64]{2,0,1:T(8,128)(2,1)S(1)} %get-tuple-element.494), kind=kLoop, calls=%fused_computation.22 | loop fusion | flops 5242880 | bytes 5242880 | tf_op jit(solution)/shard_map/concatenate | solution.py:31
  28.9 39.6 %all-gather.2.cloned.1.call-done = bf16[2048,2048]{0,1:T(8,128)(2,1)} async-done(((bf16[256,2048]{0,1:T(8,128)(2,1)}), bf16[2048,2048]{0,1:T(8,128)(2,1)}) %all-gather.2.cloned.1.call-update) | async-done | bytes 8388624 | tf_op jit(solution)/shard_map/all_gather | solution.py:120
  68.5 2.9 %broadcast_in_dim.122 = f32[8,5,256,128]{3,2,1,0:T(8,128)} broadcast(f32[]{:T(128)} %constant.102.clone.1), dimensions={} | broadcast | bytes 5242884 | tf_op jit(solution)/shard_map/broadcast_in_dim | solution.py:99
  71.4 92.3 %while.22 = (s32[]{:T(128)}, f32[8,5,256]{2,1,0:T(8,128)S(1)}, f32[8,5,256]{2,1,0:T(8,128)S(1)}, f32[8,5,256,128]{3,2,1,0:T(8,128)}, s32[]{:T(128)}, /*index=5*/...) while((s32[]{:T(128)}, f32[8,5,256]{2,1,0:T(8,128)S(1)}, ...), condition=%wide.region_8.9_spmd.clone, body=%wide.region_3.8_spmd.clone.sunk | while | flops 2755547904 | bytes 171582896 | solution.py:94
  74.0 29.0 %conditional.3 = ((f32[8,5,256]{2,1,0:T(8,128)S(1)}, f32[8,5,256]{2,1,0:T(8,128)S(1)}, f32[8,5,256,128]{3,2,1,0:T(8,128)})) conditional(s32[]{:T(128)} %convert_element_type.82, (f32[8,5,256]{2,1,0:T(8,128)S(1)}, f32[8,5,256]{2,1,0:T(8,128)S(1)}, f32[8,5,256,128]{3,2,1,0:T(8,128)}) %tuple.77, (s32[]{:T(128)}, s32[]{:T(128)}, s32[256]{0:T(256)S(1)}, ...), branch_computations={%region_4.4_spmd, %region_5.7_spmd} | conditional | flops 2755547904 | bytes 171581600 | solution.py:92
  74.0 0.2 compare_and_fusion
  74.2 2.7 %fusion.15 = (bf16[512,1024]{0,1:T(8,128)(2,1)}, bf16[512,1024]{0,1:T(8,128)(2,1)S(1)}) fusion(bf16[2048,2048]{0,1:T(8,128)(2,1)} %get-tuple-element.417, s32[]{:T(128)S(6)} %select_n.46, s32[]{:T(128)S(6)} %add.114), kind=kLoop, calls=%fused_computation.35 | loop fusion | bytes 4194312 | tf_op jit(solution)/shard_map/while/body/eval_jaxpr/slice | solution.py:83
  76.9 5.1 %fusion.2 = (f32[8,5,256]{2,1,0:T(8,128)S(1)}, f32[8,512,256,5]{2,1,3,0:T(8,128)S(1)}) fusion(pred[256,512]{0,1:T(8,128)(4,1)S(1)} %compare_and_fusion, bf16[512,8,128,1]{0,2,3,1:T(8,128)(2,1)S(1)} %bitcast.42, bf16[256,8,5,128]{3,0,2,1:T(8,128)(2,1)} %get-tuple-element.418), kind=kOutput, calls=%fused_computation.3 | convolution fusion | flops 1357895680 | bytes 24813568 | tf_op jit(solution)/shard_map/while/body/eval_jaxpr/cond/branch_1_fun/rhgd,bhd->hgrb/dot_general | solution.py:57
  82.0 0.0 copy-start
  82.1 0.0 copy-start.1
  82.1 5.0 %fusion.4 = f32[8,5,256]{2,1,0:T(8,128)S(1)} fusion(f32[8,512,256,5]{2,1,3,0:T(8,128)S(1)} %get-tuple-element.493, f32[8,5,256]{2,1,0:T(8,128)S(1)} %max.4, pred[256,512]{0,1:T(8,128)(4,1)S(1)} %compare_and_fusion), kind=kLoop, calls=%fused_computation.5 | loop fusion | flops 26204160 | bytes 21184512 | tf_op jit(solution)/shard_map/while/body/eval_jaxpr/cond/branch_1_fun/reduce_sum | solution.py:66
  87.1 2.2 %copy-done = f32[8,512,256,5]{2,1,3,0:T(8,128)} copy-done((f32[8,512,256,5]{2,1,3,0:T(8,128)}, f32[8,512,256,5]{2,1,3,0:T(8,128)S(1)}, u32[]{:S(2)}) %copy-start) | copy-done | bytes 20971544 | tf_op jit(solution)/shard_map/while/body/eval_jaxpr/cond
  89.4 0.0 copy-done.1
  89.4 13.6 %multiply_add_fusion = f32[8,5,256,128]{3,2,1,0:T(8,128)} fusion(f32[8,5,256,128]{3,2,1,0:T(8,128)} %get-tuple-element.420, f32[8,5,256]{2,1,0:T(8,128)S(1)} %get-tuple-element.489, bf16[512,8,128,1]{0,2,3,1:T(8,128)(2,1)S(1)} %bitcast.44, f32[8,512,256,5]{2,1,3,0:T(8,128)} %copy-done, f32[8,5,256]{2,1,0:T(8,128)S(1)} %max.4, ...), kind=kOutput, calls=%fused_computation.8 | convolution fusion | flops 1371013120 | bytes 32718848 | tf_op jit(solution)/shard_map/while/body/eval_jaxpr/cond/branch_1_fun/hgrb,bhd->hgrd/dot_general | solution.py:67
  104.3 29.0 %conditional.3 = ((f32[8,5,256]{2,1,0:T(8,128)S(1)}, f32[8,5,256]{2,1,0:T(8,128)S(1)}, f32[8,5,256,128]{3,2,1,0:T(8,128)})) conditional(s32[]{:T(128)} %convert_element_type.82, (f32[8,5,256]{2,1,0:T(8,128)S(1)}, f32[8,5,256]{2,1,0:T(8,128)S(1)}, f32[8,5,256,128]{3,2,1,0:T(8,128)}) %tuple.77, (s32[]{:T(128)}, s32[]{:T(128)}, s32[256]{0:T(256)S(1)}, ...), branch_computations={%region_4.4_spmd, %region_5.7_spmd} | conditional | flops 2755547904 | bytes 171581600 | solution.py:92
  104.3 0.2 compare_and_fusion
  104.5 2.7 %fusion.15 = (bf16[512,1024]{0,1:T(8,128)(2,1)}, bf16[512,1024]{0,1:T(8,128)(2,1)S(1)}) fusion(bf16[2048,2048]{0,1:T(8,128)(2,1)} %get-tuple-element.417, s32[]{:T(128)S(6)} %select_n.46, s32[]{:T(128)S(6)} %add.114), kind=kLoop, calls=%fused_computation.35 | loop fusion | bytes 4194312 | tf_op jit(solution)/shard_map/while/body/eval_jaxpr/slice | solution.py:83
  107.2 5.1 %fusion.2 = (f32[8,5,256]{2,1,0:T(8,128)S(1)}, f32[8,512,256,5]{2,1,3,0:T(8,128)S(1)}) fusion(pred[256,512]{0,1:T(8,128)(4,1)S(1)} %compare_and_fusion, bf16[512,8,128,1]{0,2,3,1:T(8,128)(2,1)S(1)} %bitcast.42, bf16[256,8,5,128]{3,0,2,1:T(8,128)(2,1)} %get-tuple-element.418), kind=kOutput, calls=%fused_computation.3 | convolution fusion | flops 1357895680 | bytes 24813568 | tf_op jit(solution)/shard_map/while/body/eval_jaxpr/cond/branch_1_fun/rhgd,bhd->hgrb/dot_general | solution.py:57
  112.3 0.0 copy-start
  112.4 0.0 copy-start.1
  112.4 5.0 %fusion.4 = f32[8,5,256]{2,1,0:T(8,128)S(1)} fusion(f32[8,512,256,5]{2,1,3,0:T(8,128)S(1)} %get-tuple-element.493, f32[8,5,256]{2,1,0:T(8,128)S(1)} %max.4, pred[256,512]{0,1:T(8,128)(4,1)S(1)} %compare_and_fusion), kind=kLoop, calls=%fused_computation.5 | loop fusion | flops 26204160 | bytes 21184512 | tf_op jit(solution)/shard_map/while/body/eval_jaxpr/cond/branch_1_fun/reduce_sum | solution.py:66
  117.4 2.2 %copy-done = f32[8,512,256,5]{2,1,3,0:T(8,128)} copy-done((f32[8,512,256,5]{2,1,3,0:T(8,128)}, f32[8,512,256,5]{2,1,3,0:T(8,128)S(1)}, u32[]{:S(2)}) %copy-start) | copy-done | bytes 20971544 | tf_op jit(solution)/shard_map/while/body/eval_jaxpr/cond
  119.7 0.0 copy-done.1
  119.7 13.6 %multiply_add_fusion = f32[8,5,256,128]{3,2,1,0:T(8,128)} fusion(f32[8,5,256,128]{3,2,1,0:T(8,128)} %get-tuple-element.420, f32[8,5,256]{2,1,0:T(8,128)S(1)} %get-tuple-element.489, bf16[512,8,128,1]{0,2,3,1:T(8,128)(2,1)S(1)} %bitcast.44, f32[8,512,256,5]{2,1,3,0:T(8,128)} %copy-done, f32[8,5,256]{2,1,0:T(8,128)S(1)} %max.4, ...), kind=kOutput, calls=%fused_computation.8 | convolution fusion | flops 1371013120 | bytes 32718848 | tf_op jit(solution)/shard_map/while/body/eval_jaxpr/cond/branch_1_fun/hgrb,bhd->hgrd/dot_general | solution.py:67
  134.6 29.1 %conditional.3 = ((f32[8,5,256]{2,1,0:T(8,128)S(1)}, f32[8,5,256]{2,1,0:T(8,128)S(1)}, f32[8,5,256,128]{3,2,1,0:T(8,128)})) conditional(s32[]{:T(128)} %convert_element_type.82, (f32[8,5,256]{2,1,0:T(8,128)S(1)}, f32[8,5,256]{2,1,0:T(8,128)S(1)}, f32[8,5,256,128]{3,2,1,0:T(8,128)}) %tuple.77, (s32[]{:T(128)}, s32[]{:T(128)}, s32[256]{0:T(256)S(1)}, ...), branch_computations={%region_4.4_spmd, %region_5.7_spmd} | conditional | flops 2755547904 | bytes 171581600 | solution.py:92
  134.7 0.2 compare_and_fusion
  134.8 2.7 %fusion.15 = (bf16[512,1024]{0,1:T(8,128)(2,1)}, bf16[512,1024]{0,1:T(8,128)(2,1)S(1)}) fusion(bf16[2048,2048]{0,1:T(8,128)(2,1)} %get-tuple-element.417, s32[]{:T(128)S(6)} %select_n.46, s32[]{:T(128)S(6)} %add.114), kind=kLoop, calls=%fused_computation.35 | loop fusion | bytes 4194312 | tf_op jit(solution)/shard_map/while/body/eval_jaxpr/slice | solution.py:83
  137.5 5.1 %fusion.2 = (f32[8,5,256]{2,1,0:T(8,128)S(1)}, f32[8,512,256,5]{2,1,3,0:T(8,128)S(1)}) fusion(pred[256,512]{0,1:T(8,128)(4,1)S(1)} %compare_and_fusion, bf16[512,8,128,1]{0,2,3,1:T(8,128)(2,1)S(1)} %bitcast.42, bf16[256,8,5,128]{3,0,2,1:T(8,128)(2,1)} %get-tuple-element.418), kind=kOutput, calls=%fused_computation.3 | convolution fusion | flops 1357895680 | bytes 24813568 | tf_op jit(solution)/shard_map/while/body/eval_jaxpr/cond/branch_1_fun/rhgd,bhd->hgrb/dot_general | solution.py:57
  142.7 0.0 copy-start
  142.7 0.0 copy-start.1
  142.7 5.0 %fusion.4 = f32[8,5,256]{2,1,0:T(8,128)S(1)} fusion(f32[8,512,256,5]{2,1,3,0:T(8,128)S(1)} %get-tuple-element.493, f32[8,5,256]{2,1,0:T(8,128)S(1)} %max.4, pred[256,512]{0,1:T(8,128)(4,1)S(1)} %compare_and_fusion), kind=kLoop, calls=%fused_computation.5 | loop fusion | flops 26204160 | bytes 21184512 | tf_op jit(solution)/shard_map/while/body/eval_jaxpr/cond/branch_1_fun/reduce_sum | solution.py:66
  147.8 2.2 %copy-done = f32[8,512,256,5]{2,1,3,0:T(8,128)} copy-done((f32[8,512,256,5]{2,1,3,0:T(8,128)}, f32[8,512,256,5]{2,1,3,0:T(8,128)S(1)}, u32[]{:S(2)}) %copy-start) | copy-done | bytes 20971544 | tf_op jit(solution)/shard_map/while/body/eval_jaxpr/cond
  150.0 0.0 copy-done.1
  150.0 13.6 %multiply_add_fusion = f32[8,5,256,128]{3,2,1,0:T(8,128)} fusion(f32[8,5,256,128]{3,2,1,0:T(8,128)} %get-tuple-element.420, f32[8,5,256]{2,1,0:T(8,128)S(1)} %get-tuple-element.489, bf16[512,8,128,1]{0,2,3,1:T(8,128)(2,1)S(1)} %bitcast.44, f32[8,512,256,5]{2,1,3,0:T(8,128)} %copy-done, f32[8,5,256]{2,1,0:T(8,128)S(1)} %max.4, ...), kind=kOutput, calls=%fused_computation.8 | convolution fusion | flops 1371013120 | bytes 32718848 | tf_op jit(solution)/shard_map/while/body/eval_jaxpr/cond/branch_1_fun/hgrb,bhd->hgrd/dot_general | solution.py:67
  163.7 5.9 %copy.32 = f32[8,5,256,128]{2,3,1,0:T(8,128)} copy(f32[8,5,256,128]{3,2,1,0:T(8,128)} %get-tuple-element.437) | data formatting | bytes 10485760 | tf_op jit(solution)/shard_map/while | solution.py:94
  169.6 3.1 %divide_convert_fusion = bf16[8,5,256,128]{2,3,1,0:T(8,128)(2,1)S(1)} fusion(f32[8,5,256,128]{2,3,1,0:T(8,128)} %copy.32, f32[8,5,256]{2,1,0:T(8,128)S(1)} %get-tuple-element.438), kind=kLoop, calls=%fused_computation.19 | loop fusion | flops 2621440 | bytes 7905280 | tf_op jit(solution)/shard_map/convert_element_type | solution.py:106
  172.7 2.8 %copy.33 = bf16[256,5120]{1,0:T(8,128)(2,1)} copy(bf16[256,5120]{0,1:T(8,128)(2,1)S(1)} %bitcast.45) | data formatting | bytes 5242880 | tf_op jit(solution)/shard_map/convert_element_type | solution.py:106
  (27 shorter events, 0.3 us)
Async XLA Ops:
  6.5 61.9 %all-gather.2.cloned.1.call-start = ((), (), s32[]{:S(2)}) async-start(), calls=%async_computation | async-start | bytes 9437184 | tf_op jit(solution)/shard_map/all_gather | solution.py:120
  10.7 2.1 %copy-start.2 = (bf16[256,5120]{1,0:T(8,128)(2,1)S(1)}, bf16[256,5120]{1,0:T(8,128)(2,1)}, u32[]{:S(2)}) copy-start(bf16[256,5120]{1,0:T(8,128)(2,1)} %param.9) | copy-start | bytes 7864324
  13.4 3.2 %copy-start.3 = (s32[8]{0:T(128)S(1)}, s32[8]{0:T(128)}, u32[]{:S(2)}) copy-start(s32[8]{0:T(128)} %param.13) | copy-start | bytes 100
  82.0 7.3 %copy-start = (f32[8,512,256,5]{2,1,3,0:T(8,128)}, f32[8,512,256,5]{2,1,3,0:T(8,128)S(1)}, u32[]{:S(2)}) copy-start(f32[8,512,256,5]{2,1,3,0:T(8,128)S(1)} %get-tuple-element.493) | copy-start | bytes 62914564 | tf_op jit(solution)/shard_map/while/body/eval_jaxpr/cond
  82.1 7.3 %copy-start.1 = (bf16[512,1024]{0,1:T(8,128)(2,1)S(1)}, bf16[512,1024]{0,1:T(8,128)(2,1)}, u32[]{:S(2)}) copy-start(bf16[512,1024]{0,1:T(8,128)(2,1)} %get-tuple-element.490) | copy-start | bytes 3145732 | tf_op jit(solution)/shard_map/while/body/eval_jaxpr/cond
  112.3 7.3 %copy-start = (f32[8,512,256,5]{2,1,3,0:T(8,128)}, f32[8,512,256,5]{2,1,3,0:T(8,128)S(1)}, u32[]{:S(2)}) copy-start(f32[8,512,256,5]{2,1,3,0:T(8,128)S(1)} %get-tuple-element.493) | copy-start | bytes 62914564 | tf_op jit(solution)/shard_map/while/body/eval_jaxpr/cond
  112.4 7.3 %copy-start.1 = (bf16[512,1024]{0,1:T(8,128)(2,1)S(1)}, bf16[512,1024]{0,1:T(8,128)(2,1)}, u32[]{:S(2)}) copy-start(bf16[512,1024]{0,1:T(8,128)(2,1)} %get-tuple-element.490) | copy-start | bytes 3145732 | tf_op jit(solution)/shard_map/while/body/eval_jaxpr/cond
  142.7 7.3 %copy-start = (f32[8,512,256,5]{2,1,3,0:T(8,128)}, f32[8,512,256,5]{2,1,3,0:T(8,128)S(1)}, u32[]{:S(2)}) copy-start(f32[8,512,256,5]{2,1,3,0:T(8,128)S(1)} %get-tuple-element.493) | copy-start | bytes 62914564 | tf_op jit(solution)/shard_map/while/body/eval_jaxpr/cond
  142.7 7.3 %copy-start.1 = (bf16[512,1024]{0,1:T(8,128)(2,1)S(1)}, bf16[512,1024]{0,1:T(8,128)(2,1)}, u32[]{:S(2)}) copy-start(bf16[512,1024]{0,1:T(8,128)(2,1)} %get-tuple-element.490) | copy-start | bytes 3145732 | tf_op jit(solution)/shard_map/while/body/eval_jaxpr/cond
Sparse Core Ops, SparseCore 0:
  12.0 56.4 all-gather.1
where the time goes:
time: 183 us; the launch traced here: 182 us
  matrix products  56.2 us (31%)
  waiting for transfers between devices  39.6 us (22%)
  local copies, waits for them, and re-layouts  39.5 us (22%)
  other arithmetic  28 us (15%)
  between operations  13.5 us (7%)
  loops' own time  5.4 us (3%)
    dot_general x3, matrix products, update(): jnp.einsum('hgrb,bhd->hgrd', weights.astype(jnp.bfloat16), values_blk, pr...  40.9 us
    all_gather x1, waiting for transfers between devices, fold_all(): lax.all_gather(paired, ('blk', 'uly'), axis=0, tiled=True)  39.6 us
    dot_general x3, matrix products, update(): jnp.einsum('rhgd,bhd->hgrb', grouped_query, keys_blk, preferred_element_t...  15.4 us
    reduce_sum x3, other arithmetic, update(): total = total * factor + jnp.sum(weights, axis=-1)  15.1 us
    slice x3, local copies, waits for them, and re-layouts, step(): values_blk = slab[:, kheads * HEAD_SIZE:].reshape(block, kheads, HEAD_SIZE)  8.12 us
    cond x15, local copies, waits for them, and re-layouts  6.68 us
    slice x1, local copies, waits for them, and re-layouts, apply_rotary(): lower = parts[..., :half]  6.28 us
    while x1, local copies, waits for them, and re-layouts, fold_piece(): return lax.fori_loop(0, count // block, step, carry)  5.9 us
  transfers between devices with their start and end apart: 1, of which 1 were waited for; matrix products, arithmetic and copies ran while one was open for 9% of the time, Pallas kernels for 0%

commit v1 on v0

v1 whole, which is shorter than its diff:
```python
import functools
import math

import jax
import jax.numpy as jnp
from jax import lax
from jax.experimental import pallas as pl
from jax.experimental.pallas import tpu as pltpu
from jax.sharding import PartitionSpec as P

HEAD_SIZE = 128
QUERY_PER_KEY = 5
AHEAD = 3


def rotary_tables(pos):
    half = HEAD_SIZE // 2
    pair = jnp.arange(half, dtype=jnp.int32)
    freq = jnp.power(jnp.float32(1000000.0), -2.0 * pair.astype(jnp.float32) / HEAD_SIZE)
    place = pos.astype(jnp.float32)
    first = HEAD_SIZE // 8
    second = first + 3 * HEAD_SIZE // 16
    chosen = jnp.where(
        pair[None, :] < first,
        place[0][:, None],
        jnp.where(pair[None, :] < second, place[1][:, None], place[2][:, None]),
    )
    angle = chosen * freq[None, :]
    cosine = jnp.cos(angle)
    sine = jnp.sin(angle)
    return jnp.concatenate([cosine, cosine], axis=1), jnp.concatenate([-sine, sine], axis=1)


def routes(blocks, lanes):
    count = blocks * lanes
    window = count // 2

    def place(r):
        return (r // lanes // 2, r % lanes), r // lanes % 2

    def member(chip, core):
        return (chip[0] * 2 + core) * lanes + chip[1]

    found = {}
    for s in range(count):
        home, own_core = place(s)
        wanting = set(range(s + 1, min(count, s + window + 1)))

        def entry(chip):
            if chip == home:
                return s
            for core in (own_core, 1 - own_core):
                if member(chip, core) in wanting:
                    return member(chip, core)
            return None

        for half in (0, 1):
            for r in sorted(wanting):
                chip, _ = place(r)
                source = entry(chip)
                if source == r:
                    options = []
                    if chip[1] != home[1]:
                        options.append(entry((chip[0], home[1])))
                    if chip[0] > home[0]:
                        options.append(entry((chip[0] - 1, chip[1])))
                    if half:
                        options.reverse()
                    options = [o for o in options if o is not None] + [s]
                    source = options[0]
                found.setdefault((source - s, r - source), (set(), set()))[half].add(source)
    return sorted(found.items(), key=lambda item: (-item[0][0], item[0][1]))


def among(me, devices):
    hit = jnp.bool_(False)
    for device in sorted(devices):
        hit = hit | (me == device)
    return hit


def kernel(
    plan, lanes, count, window, kheads,
    lengths, cosine, sine, keys, values, queries, out,
    kv, qbuf, obuf, bias, q_sem, o_sem, send_sem, recv_sem,
):
    rows = keys.shape[0]
    size = HEAD_SIZE
    group = QUERY_PER_KEY * size
    me = lax.axis_index("blk") * lanes + lax.axis_index("uly")
    fetch = pltpu.make_async_copy(queries, qbuf, q_sem)
    fetch.start()

    def where_is(r):
        return {"blk": lax.div(r, lanes), "uly": lax.rem(r, lanes)}

    def column(h, width):
        return pl.ds(pl.multiple_of(h * width, width), width)

    def fill_ones(i, carry):
        kv[lax.div(i, kheads), lax.rem(i, kheads), :, 2 * size:] = jnp.ones((rows, size), kv.dtype)
        return carry

    lax.fori_loop(0, (window + 1) * kheads, fill_ones, 0)
    for slot in range(1, window + 1):
        @pl.when(me < slot)
        def _():
            def clear(h, carry):
                kv[slot, h, :, : 2 * size] = jnp.zeros((rows, 2 * size), kv.dtype)
                return carry

            lax.fori_loop(0, kheads, clear, 0)

    barrier = pltpu.get_barrier_semaphore()
    for offset in range(1, count):
        peer = lax.rem(me + offset, count)
        pl.semaphore_signal(
            barrier, inc=1, device_id=where_is(peer), device_id_type=pl.DeviceIdType.MESH
        )

    def turn(x):
        x = x.astype(jnp.float32)
        return (x * cosine[...] + pltpu.roll(x, size // 2, 1) * sine[...]).astype(jnp.bfloat16)

    def own_block(h, carry):
        kv[0, h, :, :size] = turn(keys[:, column(h, size)])
        kv[0, h, :, size : 2 * size] = values[:, column(h, size)]
        return carry

    lax.fori_loop(0, kheads, own_block, 0)
    pl.semaphore_wait(barrier, count - 1)

    def copy_of(index, slot, step, h):
        return pltpu.make_async_remote_copy(
            src_ref=kv.at[slot, h, :, pl.ds(0, 2 * size)],
            dst_ref=kv.at[slot + step, h, :, pl.ds(0, 2 * size)],
            send_sem=send_sem.at[index, h],
            recv_sem=recv_sem.at[slot + step, h],
            device_id=where_is(me + step),
            device_id_type=pl.DeviceIdType.MESH,
        )

    def arrival(slot, h):
        return pltpu.make_async_remote_copy(
            src_ref=kv.at[slot, h, :, pl.ds(0, 2 * size)],
            dst_ref=kv.at[slot, h, :, pl.ds(0, 2 * size)],
            send_sem=send_sem.at[0, h],
            recv_sem=recv_sem.at[slot, h],
            device_id=where_is(me),
            device_id_type=pl.DeviceIdType.MESH,
        )

    def sends(senders, h):
        even, odd = senders
        if even == odd:
            return among(me, even)
        is_even = lax.rem(h, 2) == 0
        return (is_even & among(me, even)) | (jnp.logical_not(is_even) & among(me, odd))

    def send(slot, h):
        for index, ((from_slot, step), senders) in enumerate(plan):
            if from_slot == slot:
                @pl.when(sends(senders, h))
                def _():
                    copy_of(index, slot, step, h).start()

    def relays(slot, h):
        hit = jnp.bool_(False)
        for (from_slot, _), senders in plan:
            if from_slot == slot:
                hit = hit | sends(senders, h)
        return hit

    def first_sends(h, carry):
        send(0, h)
        return carry

    lax.fori_loop(0, AHEAD, first_sends, 0)

    row = lax.broadcasted_iota(jnp.int32, (rows, rows), 0) + me * rows
    col = lax.broadcasted_iota(jnp.int32, (rows, rows), 1)
    start = jnp.zeros((rows, rows), jnp.int32)
    end = jnp.int32(0)
    for d in range(lengths.shape[0]):
        end = end + lengths[d]
        start = start + jnp.where(row >= end, lengths[d], 0)
    for slot in range(window + 1):
        key = col + (me - slot) * rows
        allowed = (key >= start) & (key <= row)
        bias[:, slot * rows : (slot + 1) * rows] = jnp.where(allowed, 0.0, -1e30)

    fetch.wait()
    scale = math.log2(math.e) / math.sqrt(size)

    def head(h, carry):
        @pl.when(h + AHEAD < kheads)
        def _():
            send(0, h + AHEAD)

        for slot in range(window, 0, -1):
            @pl.when(relays(slot, h))
            def _():
                arrival(slot, h).wait_recv()
                send(slot, h)

        for slot in range(1, window + 1):
            @pl.when((me >= slot) & jnp.logical_not(relays(slot, h)))
            def _():
                arrival(slot, h).wait_recv()

        k_all = kv[:, h, :, :size].reshape((window + 1) * rows, size)
        v_all = kv[:, h, :, size:].reshape((window + 1) * rows, 2 * size)
        for g in range(QUERY_PER_KEY):
            at = pl.ds(pl.multiple_of(h * group + g * size, size), size)
            q = turn(qbuf[:, at])
            scores = lax.dot_general(
                q, k_all, (((1,), (1,)), ((), ())), preferred_element_type=jnp.float32
            )
            scores = scores + bias[...]
            best = jnp.max(scores, axis=1, keepdims=True)
            weights = jnp.exp2((scores - best) * scale).astype(jnp.bfloat16)
            summed = jnp.dot(weights, v_all, preferred_element_type=jnp.float32)
            obuf[:, at] = (summed[:, :size] / summed[:, size:]).astype(jnp.bfloat16)
        pltpu.make_async_copy(
            obuf.at[:, column(h, group)], out.at[:, column(h, group)], o_sem.at[h]
        ).start()
        return carry

    lax.fori_loop(0, kheads, head, 0)

    def finish(h, carry):
        for index, ((slot, step), senders) in enumerate(plan):
            @pl.when(sends(senders, h))
            def _():
                copy_of(index, slot, step, h).wait_send()

        pltpu.make_async_copy(
            obuf.at[:, column(h, group)], out.at[:, column(h, group)], o_sem.at[h]
        ).wait()
        return carry

    lax.fori_loop(0, kheads, finish, 0)


def local(blocks, lanes, queries, keys, values, positions, doc_lengths):
    rows = queries.shape[0]
    kheads = keys.shape[1] // HEAD_SIZE
    count = blocks * lanes
    window = count // 2
    plan = routes(blocks, lanes)
    cosine, sine = rotary_tables(positions)
    vmem = pl.BlockSpec(memory_space=pltpu.VMEM)
    anywhere = pl.BlockSpec(memory_space=pl.ANY)
    return pl.pallas_call(
        functools.partial(kernel, plan, lanes, count, window, kheads),
        out_shape=jax.ShapeDtypeStruct(queries.shape, jnp.bfloat16),
        in_specs=[pl.BlockSpec(memory_space=pltpu.SMEM), vmem, vmem, vmem, vmem, anywhere],
        out_specs=anywhere,
        scratch_shapes=[
            pltpu.VMEM((window + 1, kheads, rows, 3 * HEAD_SIZE), jnp.bfloat16),
            pltpu.VMEM(queries.shape, jnp.bfloat16),
            pltpu.VMEM(queries.shape, jnp.bfloat16),
            pltpu.VMEM((rows, (window + 1) * rows), jnp.float32),
            pltpu.SemaphoreType.DMA,
            pltpu.SemaphoreType.DMA((kheads,)),
            pltpu.SemaphoreType.DMA((len(plan), kheads)),
            pltpu.SemaphoreType.DMA((window + 1, kheads)),
        ],
        compiler_params=pltpu.CompilerParams(
            collective_id=0, has_side_effects=True, vmem_limit_bytes=60 * 1024 * 1024
        ),
        name="windowed_attention",
    )(doc_lengths, cosine, sine, keys, values, queries)


def solution(mesh):
    in_specs = (
        P(("seq", "blk", "uly"), None),
        P(("seq", "blk", "uly"), None),
        P(("seq", "blk", "uly"), None),
        P(None, ("seq", "blk", "uly")),
        P("seq"),
    )
    out_specs = P(("seq", "blk", "uly"), None)
    body = functools.partial(local, mesh.shape["blk"], mesh.shape["uly"])
    return jax.shard_map(body, mesh=mesh, in_specs=in_specs, out_specs=out_specs, check_vma=False)
```

time: 183 us -> 67.7 us (0.37)
  Pallas kernels: 0 us -> 61.1 us
  matrix products: 56.2 us -> 0 us
  waiting for transfers between devices: 39.6 us -> 0 us
  local copies, waits for them, and re-layouts: 39.5 us -> 3.41 us
  other arithmetic: 28 us -> 2.16 us
  between operations: 13.5 us -> 0.02 us
  loops' own time: 5.4 us -> 0 us
    pallas_call x0 -> x1, Pallas kernels: none -> 61.1 us  [local(): pl.pallas_call(functools.partial(kernel, plan, lanes, count, window, khea...]
    dot_general x6 -> x0, matrix products: 56.2 us -> none  [the longest x3 40.9 us: update(): jnp.einsum('hgrb,bhd->hgrd', weights.astype(jnp.bfloat16), values_blk, pr...]
    all_gather x1 -> x0, waiting for transfers between devices: 39.6 us -> none  [fold_all(): lax.all_gather(paired, ('blk', 'uly'), axis=0, tiled=True)]
    reduce_sum x4 -> x0, other arithmetic: 15.2 us -> none  [the longest x3 15.1 us: update(): total = total * factor + jnp.sum(weights, axis=-1)]
    slice x6 -> x1, local copies, waits for them, and re-layouts: 15.1 us -> 0.01 us  [rotary_tables(): place[0][:, None]]
    cond x15 -> x0, local copies, waits for them, and re-layouts: 6.68 us -> none
    while x1 -> x0, local copies, waits for them, and re-layouts: 5.9 us -> none  [fold_piece(): return lax.fori_loop(0, count // block, step, carry)]
    another operation x5 -> x0, loops' own time: 5.4 us -> none  [the longest x1 5.09 us: fold_piece(): return lax.fori_loop(0, count // block, step, carry)]
  transfers between devices with their start and end apart: 1 -> 0, of which waited for: 1 -> 0; matrix products, arithmetic and copies ran while one was open for 9% -> 0% of each run, Pallas kernels for 0% -> 0%
where the time goes in v1:
time: 67.7 us; the launch traced here: 66.7 us
  Pallas kernels  61.1 us (90%)
  local copies, waits for them, and re-layouts  3.41 us (5%)
  other arithmetic  2.16 us (3%)
    pallas_call x1, Pallas kernels, local(): pl.pallas_call(functools.partial(kernel, plan, lanes, count, window, khea...  61.1 us
    unnamed x1, local copies, waits for them, and re-layouts  3.4 us

profile of v1, /device:TPU:13, one launch (start us, length us, event | category | flops | bytes accessed | tf_op | source)
XLA Modules:
  0.0 66.7 jit_solution(8567123430078094594)
XLA Ops:
  0.0 0.7 %convert_element_type.10 = f32[3,256]{1,0:T(4,128)S(1)} convert(s32[3,256]{1,0:T(4,128)} %param.8) | non-fusion elementwise | flops 768 | bytes 6144 | tf_op jit(solution)/shard_map/convert_element_type | solution.py:20
  0.7 0.6 fusion.2
  1.3 0.8 %pad_maximum_fusion = (f32[256,128]{1,0:T(8,128)}, f32[256,128]{1,0:T(8,128)}) fusion(f32[256,64]{1,0:T(8,128)S(1)} %get-tuple-element.7, f32[256,64]{1,0:T(8,128)S(1)} %get-tuple-element.6, f32[256,64]{1,0:T(8,128)S(1)} %get-tuple-element.5), kind=kLoop, calls=%fused_computation | loop fusion | flops 65536 | bytes 458752 | tf_op jit(solution)/shard_map/concatenate | solution.py:31
  2.2 61.1 %windowed_attention.1 = bf16[256,5120]{1,0:T(8,128)(2,1)} custom-call(s32[8]{0:T(128)} %lengths.1, f32[256,128]{1,0:T(8,128)} %get-tuple-element.11.cosine, f32[256,128]{1,0:T(8,128)} %get-tuple-element.12.sine, bf16[256,1024]{1,0:T(8,128)(2,1)} %keys.1, bf16[256,1024]{1,0:T(8,128)(2,1)} %values.1, bf16[256,5120]{1,0:T(8,128)(2,1)} %queries.1), custom_call_target="tpu_custom_call" | custom-call | tf_op jit(solution)/shard_map/windowed_attention/pallas_call | solution.py:254
  63.3 3.4 %copy.7 = bf16[256,5120]{1,0:T(8,128)(2,1)} copy(bf16[256,5120]{1,0:T(8,128)(2,1)} %windowed_attention.1) | data formatting | bytes 5242880
  (4 shorter events, 0.0 us)

commit v2 on v1

--- a/solution.py
+++ b/solution.py
@@ -3,6 +3,7 @@
 
 import jax
 import jax.numpy as jnp
+import numpy as np
 from jax import lax
 from jax.experimental import pallas as pl
 from jax.experimental.pallas import tpu as pltpu
@@ -11,24 +12,53 @@
 HEAD_SIZE = 128
 QUERY_PER_KEY = 5
 AHEAD = 3
-
-
-def rotary_tables(pos):
+RELAY_AHEAD = 1
+
+
+def frequencies():
+    pair = np.arange(HEAD_SIZE) % (HEAD_SIZE // 2)
+    return np.power(1000000.0, -2.0 * pair / HEAD_SIZE).astype(np.float32)[None, :]
+
+
+def rotary_tables(places, freq):
+    rows = places.shape[1]
     half = HEAD_SIZE // 2
-    pair = jnp.arange(half, dtype=jnp.int32)
-    freq = jnp.power(jnp.float32(1000000.0), -2.0 * pair.astype(jnp.float32) / HEAD_SIZE)
-    place = pos.astype(jnp.float32)
+    row = lax.broadcasted_iota(jnp.int32, (rows, rows), 0)
+    col = lax.broadcasted_iota(jnp.int32, (rows, rows), 1)
+    column = [
+        jnp.sum(
+            jnp.where(row == col, places[p : p + 1, :].astype(jnp.float32), 0.0),
+            axis=1,
+            keepdims=True,
+        )
+        for p in range(3)
+    ]
+    lane = lax.broadcasted_iota(jnp.int32, (rows, HEAD_SIZE), 1)
+    upper = lane >= half
+    pair = jnp.where(upper, lane - half, lane)
     first = HEAD_SIZE // 8
     second = first + 3 * HEAD_SIZE // 16
-    chosen = jnp.where(
-        pair[None, :] < first,
-        place[0][:, None],
-        jnp.where(pair[None, :] < second, place[1][:, None], place[2][:, None]),
+    chosen = jnp.where(pair < first, column[0], jnp.where(pair < second, column[1], column[2]))
+    angle = chosen * freq
+    turns = jnp.floor(angle * (2.0 / math.pi) + 0.5)
+    rest = angle - turns * 1.5703125
+    rest = rest - turns * 4.8351287841796875e-4
+    rest = rest - turns * 3.138552419841289520264e-7
+    rest = rest - turns * 6.07710050630396597660e-11
+    quarter = turns.astype(jnp.int32) & 3
+    square = rest * rest
+    sine = rest + rest * square * (
+        -1.0 / 6 + square * (1.0 / 120 + square * (-1.0 / 5040 + square * (1.0 / 362880)))
     )
-    angle = chosen * freq[None, :]
-    cosine = jnp.cos(angle)
-    sine = jnp.sin(angle)
-    return jnp.concatenate([cosine, cosine], axis=1), jnp.concatenate([-sine, sine], axis=1)
+    cosine = 1.0 + square * (
+        -0.5 + square * (1.0 / 24 + square * (-1.0 / 720 + square * (1.0 / 40320)))
+    )
+    swap = (quarter & 1) == 1
+    sin_turned = jnp.where(swap, cosine, sine)
+    cos_turned = jnp.where(swap, sine, cosine)
+    sin_turned = jnp.where(quarter >= 2, -sin_turned, sin_turned)
+    cos_turned = jnp.where((quarter == 1) | (quarter == 2), -cos_turned, cos_turned)
+    return cos_turned, jnp.where(upper, sin_turned, -sin_turned)
 
 
 def routes(blocks, lanes):
@@ -81,8 +111,8 @@
 
 def kernel(
     plan, lanes, count, window, kheads,
-    lengths, cosine, sine, keys, values, queries, out,
-    kv, qbuf, obuf, bias, q_sem, o_sem, send_sem, recv_sem,
+    lengths, places, freq, keys, values, queries, out,
+    cosine, sine, kv, qbuf, bias, q_sem, send_sem, recv_sem,
 ):
     rows = keys.shape[0]
     size = HEAD_SIZE
@@ -117,6 +147,8 @@
         pl.semaphore_signal(
             barrier, inc=1, device_id=where_is(peer), device_id_type=pl.DeviceIdType.MESH
         )
+
+    cosine[...], sine[...] = rotary_tables(places, freq[...])
 
     def turn(x):
         x = x.astype(jnp.float32)
@@ -176,6 +208,15 @@
         return carry
 
     lax.fori_loop(0, AHEAD, first_sends, 0)
+
+    def forward(h, carry):
+        for slot in range(window, 0, -1):
+            @pl.when(relays(slot, h))
+            def _():
+                arrival(slot, h).wait_recv()
+                send(slot, h)
+
+        return carry
 
     row = lax.broadcasted_iota(jnp.int32, (rows, rows), 0) + me * rows
     col = lax.broadcasted_iota(jnp.int32, (rows, rows), 1)
@@ -190,6 +231,7 @@
         bias[:, slot * rows : (slot + 1) * rows] = jnp.where(allowed, 0.0, -1e30)
 
     fetch.wait()
+    lax.fori_loop(0, RELAY_AHEAD, forward, 0)
     scale = math.log2(math.e) / math.sqrt(size)
 
     def head(h, carry):
@@ -197,11 +239,9 @@
         def _():
             send(0, h + AHEAD)
 
-        for slot in range(window, 0, -1):
-            @pl.when(relays(slot, h))
-            def _():
-                arrival(slot, h).wait_recv()
-                send(slot, h)
+        @pl.when(h + RELAY_AHEAD < kheads)
+        def _():
+            forward(h + RELAY_AHEAD, carry)
 
         for slot in range(1, window + 1):
             @pl.when((me >= slot) & jnp.logical_not(relays(slot, h)))
@@ -220,10 +260,7 @@
             best = jnp.max(scores, axis=1, keepdims=True)
             weights = jnp.exp2((scores - best) * scale).astype(jnp.bfloat16)
             summed = jnp.dot(weights, v_all, preferred_element_type=jnp.float32)
-            obuf[:, at] = (summed[:, :size] / summed[:, size:]).astype(jnp.bfloat16)
-        pltpu.make_async_copy(
-            obuf.at[:, column(h, group)], out.at[:, column(h, group)], o_sem.at[h]
-        ).start()
+            out[:, at] = (summed[:, :size] / summed[:, size:]).astype(jnp.bfloat16)
         return carry
 
     lax.fori_loop(0, kheads, head, 0)
@@ -234,9 +271,6 @@
             def _():
                 copy_of(index, slot, step, h).wait_send()
 
-        pltpu.make_async_copy(
-            obuf.at[:, column(h, group)], out.at[:, column(h, group)], o_sem.at[h]
-        ).wait()
         return carry
 
     lax.fori_loop(0, kheads, finish, 0)
@@ -248,21 +282,20 @@
     count = blocks * lanes
     window = count // 2
     plan = routes(blocks, lanes)
-    cosine, sine = rotary_tables(positions)
     vmem = pl.BlockSpec(memory_space=pltpu.VMEM)
     anywhere = pl.BlockSpec(memory_space=pl.ANY)
     return pl.pallas_call(
         functools.partial(kernel, plan, lanes, count, window, kheads),
-        out_shape=jax.ShapeDtypeStruct(queries.shape, jnp.bfloat16),
+        out_shape=pltpu.VMEM(queries.shape, jnp.bfloat16),
         in_specs=[pl.BlockSpec(memory_space=pltpu.SMEM), vmem, vmem, vmem, vmem, anywhere],
-        out_specs=anywhere,
+        out_specs=vmem,
         scratch_shapes=[
+            pltpu.VMEM((rows, HEAD_SIZE), jnp.float32),
+            pltpu.VMEM((rows, HEAD_SIZE), jnp.float32),
             pltpu.VMEM((window + 1, kheads, rows, 3 * HEAD_SIZE), jnp.bfloat16),
-            pltpu.VMEM(queries.shape, jnp.bfloat16),
             pltpu.VMEM(queries.shape, jnp.bfloat16),
             pltpu.VMEM((rows, (window + 1) * rows), jnp.float32),
             pltpu.SemaphoreType.DMA,
-            pltpu.SemaphoreType.DMA((kheads,)),
             pltpu.SemaphoreType.DMA((len(plan), kheads)),
             pltpu.SemaphoreType.DMA((window + 1, kheads)),
         ],
@@ -270,7 +303,7 @@
             collective_id=0, has_side_effects=True, vmem_limit_bytes=60 * 1024 * 1024
         ),
         name="windowed_attention",
-    )(doc_lengths, cosine, sine, keys, values, queries)
+    )(doc_lengths, positions, jnp.asarray(frequencies()), keys, values, queries)
 
 
 def solution(mesh):

time: 67.7 us -> 46.9 us (0.69); the launches traced: 66.7 us -> 46.8 us
  Pallas kernels: 61.1 us -> 45.3 us
  other arithmetic: 2.16 us -> 0 us
  local copies, waits for them, and re-layouts: 3.41 us -> 1.49 us
    pallas_call x1, Pallas kernels: 61.1 us -> 45.3 us  [local(): pl.pallas_call(functools.partial(kernel, plan, lanes, count, window, khea...]
    unnamed x1, local copies, waits for them, and re-layouts: 3.4 us -> 1.49 us
    concatenate x1 -> x0, other arithmetic: 0.84 us -> none  [rotary_tables(): jnp.concatenate([cosine, cosine], axis=1)]
    convert_element_type x1 -> x0, other arithmetic: 0.69 us -> none  [rotary_tables(): place = pos.astype(jnp.float32)]
where the time goes in v2:
time: 46.9 us; the launch traced here: 46.8 us
  Pallas kernels  45.3 us (97%)
  local copies, waits for them, and re-layouts  1.49 us (3%)
    pallas_call x1, Pallas kernels, local(): pl.pallas_call(functools.partial(kernel, plan, lanes, count, window, khea...  45.3 us
    unnamed x1, local copies, waits for them, and re-layouts  1.49 us

profile of v2, /device:TPU:13, one launch (start us, length us, event | category | flops | bytes accessed | tf_op | source)
XLA Modules:
  0.0 46.8 jit_solution(13163053316453070483)
XLA Ops:
  0.0 45.3 %windowed_attention.1 = bf16[256,5120]{1,0:T(8,128)(2,1)S(1)} custom-call(s32[8]{0:T(128)} %lengths.1, s32[3,256]{1,0:T(4,128)} %places.1, f32[1,128]{1,0:T(1,128)} %constant.2.clone.freq, bf16[256,1024]{1,0:T(8,128)(2,1)} %keys.1, bf16[256,1024]{1,0:T(8,128)(2,1)} %values.1, bf16[256,5120]{1,0:T(8,128)(2,1)} %queries.1), custom_call_target="tpu_custom_call" | custom-call | tf_op jit(solution)/shard_map/windowed_attention/pallas_call | solution.py:287
  45.3 1.5 %copy.8 = bf16[256,5120]{1,0:T(8,128)(2,1)} copy(bf16[256,5120]{1,0:T(8,128)(2,1)S(1)} %windowed_attention.1) | data formatting | bytes 5242880
